TPU v7x, 128 devices: a whole 4x4x4 slice. The times are simulated.
128 devices in a mesh: tile: 64 (over x, z, y), lev: 2 (over core).
Axes of the slice: x: 4, y: 4, z: 4, core: 2. Of those that a mesh axis runs over, the one named last changes fastest.
Arguments:
- increments: bfloat16 [136, 1024, 1024], P('lev', 'tile'), may hold values from -30 to 30
- projection: bfloat16 [80, 136], replicated, may hold values from -0.5 to 0.5
- helmholtz: float32 [80], P('lev'), may hold values from 0.05 to 4
Outputs:
- solution: float32 [80, 1024, 1024], P('lev', 'tile')
- residual: float32 [80, 1024, 1024], P('lev', 'tile')
All inputs are finite; a program needn't handle non-finite values.
Results may differ from a plain program's by a relative error of at most 0.00075.
Values may be sent and summed in bfloat16 or wider, within the bound.
A program may use at most 192 MiB of HBM per device.

v0:
```python
import functools

import jax
import jax.numpy as jnp
from jax import lax
from jax.experimental import pallas as pl
from jax.experimental.pallas import tpu as pltpu
from jax.sharding import PartitionSpec as P

STEPS = 8
ROWS = 16
HALO = 8
EXT = ROWS + 2 * HALO
NEAR = 4
LANES = 128
FLAT = 216
MESH = pl.DeviceIdType.MESH


def flat(level, row):
    return 32 * level - level * level + row


def kernel(dims, inc_hbm, proj_ref, helm_ref, sol_hbm, res_hbm,
           fields, inc_own, inc_far, kron, grams, far_out, far_in, coef, gather,
           lev_send, lev_recv, load_sem, near_send, near_recv, far_send, far_recv,
           red_send, red_recv, out_sem):
    tile = lax.axis_index("tile")
    lev = lax.axis_index("lev")
    tiles = lax.axis_size("tile")
    levels, _, cells = inc_own.shape
    modes = fields.shape[1]
    groups = modes // 8
    chunk = cells // 4
    cols = cells // LANES
    other = 1 - lev
    has = (tile > 0, tile < tiles - 1)
    partner = (tile - 1, tile + 1)
    f32 = jnp.float32

    loads = []
    for c in range(4):
        part = pl.ds(c * chunk, chunk)
        load = pltpu.make_async_copy(inc_hbm.at[:, :, part], inc_own.at[:, :, part], load_sem.at[c])
        load.start()
        loads.append(load)

    barrier = pltpu.get_barrier_semaphore()
    pl.semaphore_signal(barrier, inc=1, device_id={"lev": other}, device_id_type=MESH)
    for side in range(2):
        there = lax.rem(tile + (tiles - 1 if side == 0 else 1), tiles)
        pl.semaphore_signal(barrier, inc=1, device_id={"tile": there}, device_id_type=MESH)
    places = []
    for stride, size in dims:
        place = lax.rem(lax.div(tile, stride), size)
        places.append(place)
        for step in range(1, size):
            there = tile + (lax.rem(place + step, size) - place) * stride
            pl.semaphore_signal(barrier, inc=1, device_id={"tile": there}, device_id_type=MESH)
    pl.semaphore_wait(barrier, 3 + sum(size - 1 for _, size in dims))

    sends = []
    for c in range(4):
        part = pl.ds(c * chunk, chunk)
        send = pltpu.make_async_remote_copy(
            src_ref=inc_hbm.at[:, :, part], dst_ref=inc_far.at[:, :, part],
            send_sem=lev_send.at[c], recv_sem=lev_recv.at[c],
            device_id={"lev": other}, device_id_type=MESH)
        send.start()
        sends.append(send)

    wide = levels * ROWS
    table = proj_ref[...].astype(f32)
    table = jnp.where(lev == 0, table[:modes], table[modes:])
    left, right = table[:, :levels], table[:, levels:]
    own_part = jnp.where(lev == 0, left, right)
    far_part = jnp.where(lev == 0, right, left)
    spread = (lax.broadcasted_iota(jnp.int32, (levels, wide), 1) // ROWS
              == lax.broadcasted_iota(jnp.int32, (levels, wide), 0))
    spread = jnp.where(spread, 1.0, 0.0).astype(jnp.bfloat16)
    at_row = lax.broadcasted_iota(jnp.int32, (modes, wide), 1) % ROWS
    for half, part in enumerate((own_part, far_part)):
        repeated = jnp.dot(part.astype(jnp.bfloat16), spread, preferred_element_type=f32)
        for pair in range(ROWS // 2):
            both = jnp.concatenate([
                jnp.where(at_row == 2 * pair, repeated, 0.0),
                jnp.where(at_row == 2 * pair + 1, repeated, 0.0)], axis=0)
            kron[half, pl.ds(2 * modes * pair, 2 * modes), :] = both.astype(jnp.bfloat16)

    lane8 = lax.broadcasted_iota(jnp.int32, (8, LANES), 1)
    sub8 = lax.broadcasted_iota(jnp.int32, (8, LANES), 0)
    shifts = jnp.zeros((8, LANES), f32)
    for mode in range(modes):
        shifts = jnp.where((lane8 == mode // 8) & (sub8 == mode % 8), helm_ref[mode], shifts)
    scale = 4.0 / (4.0 + shifts)

    for side, base in ((0, 0), (1, EXT - HALO)):
        @pl.when(jnp.logical_not(has[side]))
        def _():
            def clear(row, carry):
                fields[row + base] = jnp.zeros((modes, cells), f32)
                return carry
            lax.fori_loop(0, HALO, clear, 0)
    grams[...] = jnp.zeros_like(grams)

    for c in range(4):
        loads[c].wait()
        part = pl.ds(c * chunk, chunk)
        first = jnp.dot(kron[0], inc_own[:, :, part].reshape(wide, chunk), preferred_element_type=f32)
        fields[pl.ds(HALO, ROWS), :, part] = first.reshape(ROWS, modes, chunk)

    def near_copy(side, d, piece):
        mine = HALO + d - 1 if side == 0 else EXT - HALO - d
        theirs = EXT - HALO - 1 + d if side == 0 else HALO - d
        part = pl.ds(0, chunk) if piece == 0 else pl.ds(chunk, cells - chunk)
        return pltpu.make_async_remote_copy(
            src_ref=fields.at[mine, :, part], dst_ref=fields.at[theirs, :, part],
            send_sem=near_send.at[side, d - 1, piece], recv_sem=near_recv.at[1 - side, d - 1, piece],
            device_id={"tile": partner[side]}, device_id_type=MESH)

    def far_copy(side, d):
        return pltpu.make_async_remote_copy(
            src_ref=far_out.at[side, d - NEAR - 1], dst_ref=far_in.at[1 - side, d - NEAR - 1],
            send_sem=far_send.at[side, d - NEAR - 1], recv_sem=far_recv.at[1 - side, d - NEAR - 1],
            device_id={"tile": partner[side]}, device_id_type=MESH)

    for c in range(4):
        sends[c].wait_recv()
        part = pl.ds(c * chunk, chunk)
        second = jnp.dot(kron[1], inc_far[:, :, part].reshape(wide, chunk), preferred_element_type=f32)
        fields[pl.ds(HALO, ROWS), :, part] += second.reshape(ROWS, modes, chunk)
        if c in (0, 3):
            for d in range(1, NEAR + 1):
                for side in range(2):
                    @pl.when(has[side])
                    def _():
                        near_copy(side, d, 0 if c == 0 else 1).start()
    half = cells // 2
    for d in range(NEAR + 1, HALO + 1):
        for side in range(2):
            mine = HALO + d - 1 if side == 0 else EXT - HALO - d
            for group in range(groups):
                rows = pl.ds(8 * group, 8)
                both = jnp.concatenate(
                    [fields[mine, rows, pl.ds(0, half)], fields[mine, rows, pl.ds(half, half)]], axis=0)
                far_out[side, d - NEAR - 1, group] = both.astype(jnp.bfloat16)

            @pl.when(has[side])
            def _():
                far_copy(side, d).start()

    lane = lax.broadcasted_iota(jnp.int32, (modes, LANES), 1)
    at_first, at_last = lane == 0, lane == LANES - 1

    def row_step(level, row, start, gram, keep=None):
        here = flat(level - 1, row)
        old = None if start else flat(level - 2, row)
        new = flat(level, row)
        turned = {}

        def turn(j):
            if j not in turned:
                value = fields[here, :, pl.ds(j * LANES, LANES)]
                turned[j] = (value, pltpu.roll(value, 1, 1), pltpu.roll(value, LANES - 1, 1))
            return turned[j]

        squares = cross = None
        for j in range(cols):
            part = pl.ds(j * LANES, LANES)
            value, right_by, left_by = turn(j)
            before = turn(j - 1)[1] if j > 0 else 0.0
            after = turn(j + 1)[2] if j < cols - 1 else 0.0
            beside = (jnp.where(at_first, before, right_by) + jnp.where(at_last, after, left_by)
                      + (fields[here - 1, :, part] + fields[here + 1, :, part]))
            result = 0.5 * beside
            if old is not None:
                result = result - fields[old, :, part]
            if keep is not None:
                result = result * keep
            fields[new, :, part] = result
            if gram:
                squares = value * value if squares is None else squares + value * value
                cross = value * result if cross is None else cross + value * result
        if gram:
            grams[2 * level - 2] += squares
            grams[2 * level - 1] += cross

    def inner(level, start):
        def pair(i, carry):
            row = HALO + level + 2 * i
            row_step(level, row, start, True)
            row_step(level, row + 1, start, True)
            return carry
        lax.fori_loop(0, HALO - level, pair, 0)

    inner(1, True)

    def inner_level(level, carry):
        inner(level, False)
        return carry

    lax.fori_loop(2, HALO, inner_level, 0)

    keeps = tuple(jnp.where(has[side], 1.0, 0.0) for side in range(2))

    def both_sides(level, d, start, gram):
        q = level - d
        row_step(level, HALO + q, start, gram, None if gram else keeps[0])
        row_step(level, EXT - HALO - 1 - q, start, gram, None if gram else keeps[1])

    def near_wait(side, d):
        for piece in range(2):
            theirs = HALO - d if side == 0 else EXT - HALO - 1 + d
            part = pl.ds(0, chunk) if piece == 0 else pl.ds(chunk, cells - chunk)
            pltpu.make_async_remote_copy(
                src_ref=fields.at[theirs, :, part], dst_ref=fields.at[theirs, :, part],
                send_sem=near_send.at[side, d - 1, piece], recv_sem=near_recv.at[side, d - 1, piece],
                device_id={"tile": partner[side]}, device_id_type=MESH).wait_recv()

    def far_wait(side, d):
        pltpu.make_async_remote_copy(
            src_ref=far_in.at[side, d - NEAR - 1], dst_ref=far_in.at[side, d - NEAR - 1],
            send_sem=far_send.at[side, d - NEAR - 1], recv_sem=far_recv.at[side, d - NEAR - 1],
            device_id={"tile": partner[side]}, device_id_type=MESH).wait_recv()
        theirs = HALO - d if side == 0 else EXT - HALO - 1 + d
        for group in range(groups):
            both = far_in[side, d - NEAR - 1, group].astype(f32)
            rows = pl.ds(8 * group, 8)
            fields[theirs, rows, pl.ds(0, half)] = both[:8]
            fields[theirs, rows, pl.ds(half, half)] = both[8:]

    def front(d, carry):
        for side in range(2):
            @pl.when(has[side] & (d <= NEAR))
            def _():
                near_wait(side, d)

            @pl.when(has[side] & (d > NEAR))
            def _():
                far_wait(side, d)

        @pl.when(d == 1)
        def _():
            both_sides(1, d, True, True)

        @pl.when(d > 1)
        def _():
            both_sides(1, d, True, False)

        def halo_level(level, c):
            both_sides(level, d, False, False)
            return c

        def own_level(level, c):
            both_sides(level, d, False, True)
            return c

        lax.fori_loop(2, d, halo_level, 0)
        lax.fori_loop(jnp.maximum(d, 2), STEPS + 1, own_level, 0)
        return carry

    lax.fori_loop(1, HALO + 1, front, 0)

    values = [grams[i] for i in range(2 * STEPS)]

    def fold(low, high, shift, lanes):
        kept = low + pltpu.roll(low, LANES - shift, 1)
        if high is None:
            high = jnp.zeros_like(low)
        moved = high + pltpu.roll(high, shift, 1)
        return jnp.where((lanes & shift) == 0, kept, moved)

    shift = LANES // 2
    while len(values) > 1:
        middle = len(values) // 2
        values = [fold(values[i], values[i + middle], shift, lane) for i in range(middle)]
        shift //= 2
    values = [values[0][8 * g:8 * g + 8] for g in range(groups)] + [None] * (8 - groups)
    while len(values) > 1:
        middle = len(values) // 2
        values = [None if values[i] is None else fold(values[i], values[i + middle], shift, lane8)
                  for i in range(middle)]
        shift //= 2
    total = values[0]

    for phase, (stride, size) in enumerate(dims):
        place = places[phase]
        gather[phase, place] = total
        copies = []
        for step in range(1, size):
            there = tile + (lax.rem(place + step, size) - place) * stride
            copy = pltpu.make_async_remote_copy(
                src_ref=gather.at[phase, place], dst_ref=gather.at[phase, place],
                send_sem=red_send.at[phase, step - 1], recv_sem=red_recv.at[phase, step - 1],
                device_id={"tile": there}, device_id_type=MESH)
            copy.start()
            copies.append(copy)
        for copy in copies:
            copy.wait_recv()
        total = gather[phase, 0]
        for i in range(1, size):
            total = total + gather[phase, i]

    dots = [total if i == 0 else pltpu.roll(total, LANES - 8 * i, 1) for i in range(2 * STEPS)]
    moments = dots[:2]
    for i in range(2, 2 * STEPS):
        moments.append(dots[i] - dots[i - 2])
    zero = jnp.zeros_like(total)
    half_scale = 0.5 * scale
    r_mom, p_mom = list(moments), list(moments)
    r_co, p_co, x_co = [zero + 1.0], [zero + 1.0], []
    squares = moments[0]

    def add(items):
        items = list(items)
        while len(items) > 1:
            items = [items[i] + items[i + 1] if i + 1 < len(items) else items[i]
                     for i in range(0, len(items), 2)]
        return items[0]

    for step in range(STEPS):
        through = []
        for i in range(len(p_mom) - 1):
            around = p_mom[i + 1] if i == 0 else p_mom[i - 1] + p_mom[i + 1]
            through.append(p_mom[i] - half_scale * around)
        alpha = squares / add(p_co[i] * through[i] for i in range(step + 1))
        x_co = [x_co[i] + alpha * p_co[i] if i < len(x_co) else alpha * p_co[i] for i in range(step + 1)]
        grown = []
        for i in range(step + 2):
            terms = [p_co[k] for k in (i - 1, i + 1) if 0 <= k <= step]
            moved = p_co[i] if i <= step else zero
            if terms:
                moved = moved - half_scale * add(terms)
            grown.append(r_co[i] - alpha * moved if i < len(r_co) else -(alpha * moved))
        r_co = grown
        if step == STEPS - 1:
            break
        r_mom = [r_mom[i] - alpha * through[i] for i in range(len(through))]
        fresh = add(r_co[i] * r_mom[i] for i in range(step + 2))
        beta = fresh / squares
        squares = fresh
        p_co = [r_co[i] + beta * p_co[i] if i <= step else r_co[i] for i in range(step + 2)]
        p_mom = [r_mom[i] + beta * p_mom[i] for i in range(len(r_mom))]

    for i, value in enumerate(x_co + r_co):
        for group in range(groups):
            coef[i, pl.ds(8 * group, 8), :] = jnp.broadcast_to(value[:, group:group + 1], (8, LANES))

    def out_copy(which, row):
        source = fields.at[flat(7 + which, HALO + row)]
        target = (sol_hbm, res_hbm)[which].at[:, row, :]
        return pltpu.make_async_copy(source, target, out_sem.at[which, row])

    def combine(pair, carry):
        def one_group(group, c):
            rows = pl.ds(pl.multiple_of(8 * group, 8), 8)
            factors = [coef[i, rows, :] for i in range(2 * STEPS + 1)]
            for more in range(2):
                row = HALO + 2 * pair + more
                for j in range(cols):
                    part = pl.ds(j * LANES, LANES)
                    parts = [fields[flat(k, row), rows, part] for k in range(STEPS + 1)]
                    sol = add(factors[k] * parts[k] for k in range(STEPS))
                    res = add(factors[STEPS + k] * parts[k] for k in range(STEPS + 1))
                    fields[flat(7, row), rows, part] = sol
                    fields[flat(8, row), rows, part] = res
            return c
        lax.fori_loop(0, groups, one_group, 0)
        for more in range(2):
            for which in range(2):
                out_copy(which, 2 * pair + more).start()
        return carry

    lax.fori_loop(0, ROWS // 2, combine, 0)

    for send in sends:
        send.wait_send()
    for side in range(2):
        @pl.when(has[side])
        def _():
            for d in range(1, NEAR + 1):
                for piece in range(2):
                    near_copy(side, d, piece).wait_send()
            for d in range(NEAR + 1, HALO + 1):
                far_copy(side, d).wait_send()
    for phase, (stride, size) in enumerate(dims):
        for step in range(1, size):
            pltpu.make_async_remote_copy(
                src_ref=gather.at[phase, places[phase]], dst_ref=gather.at[phase, places[phase]],
                send_sem=red_send.at[phase, step - 1], recv_sem=red_recv.at[phase, step - 1],
                device_id={"tile": tile}, device_id_type=MESH).wait_send()

    def drain(row, carry):
        for which in range(2):
            out_copy(which, row).wait()
        return carry

    lax.fori_loop(0, ROWS, drain, 0)


def shards(dims, increments, projection, helmholtz):
    levels, rows, cells = increments.shape
    modes = projection.shape[0] // 2
    groups = modes // 8
    out = jax.ShapeDtypeStruct((modes, rows, cells), jnp.float32)
    longest = max(size for _, size in dims)
    hbm = pl.BlockSpec(memory_space=pl.ANY)
    dma = pltpu.SemaphoreType.DMA
    return pl.pallas_call(
        functools.partial(kernel, dims),
        out_shape=(out, out),
        in_specs=[hbm, pl.BlockSpec(memory_space=pltpu.VMEM), pl.BlockSpec(memory_space=pltpu.SMEM)],
        out_specs=(hbm, hbm),
        scratch_shapes=[
            pltpu.VMEM((FLAT, modes, cells), jnp.float32),
            pltpu.VMEM((levels, rows, cells), jnp.bfloat16),
            pltpu.VMEM((levels, rows, cells), jnp.bfloat16),
            pltpu.VMEM((2, rows * modes, rows * levels), jnp.bfloat16),
            pltpu.VMEM((2 * STEPS, modes, LANES), jnp.float32),
            pltpu.VMEM((2, HALO - NEAR, groups, 16, cells // 2), jnp.bfloat16),
            pltpu.VMEM((2, HALO - NEAR, groups, 16, cells // 2), jnp.bfloat16),
            pltpu.VMEM((2 * STEPS + 1, modes, LANES), jnp.float32),
            pltpu.VMEM((len(dims), longest, 8, LANES), jnp.float32),
            dma((4,)), dma((4,)), dma((4,)),
            dma((2, NEAR, 2)), dma((2, NEAR, 2)),
            dma((2, HALO - NEAR)), dma((2, HALO - NEAR)),
            dma((len(dims), longest - 1)), dma((len(dims), longest - 1)),
            dma((2, ROWS)),
        ],
        compiler_params=pltpu.CompilerParams(
            collective_id=0, has_side_effects=True, vmem_limit_bytes=60 * 1024 * 1024),
    )(increments, projection, helmholtz)


def solution(mesh):
    tiles = mesh.shape["tile"]
    dims = ((1, 4), (4, 4), (16, 4)) if tiles == 64 else ((1, 2), (2, 2), (4, 2))
    in_specs = (P("lev", "tile", None), P(), P("lev"))
    out_specs = (P("lev", "tile", None), P("lev", "tile", None))
    return jax.shard_map(functools.partial(shards, dims), mesh=mesh, in_specs=in_specs,
                         out_specs=out_specs, check_vma=False)
```

profile of v0, /device:TPU:0, one launch (start us, length us, event | category | flops | bytes accessed | tf_op | source)
XLA Modules:
  0.0 137.0 jit_solution(6862438830033370472)
XLA Ops:
  0.6 1.5 %copy.5.proj_ref = bf16[80,136]{1,0:T(8,128)(2,1)} copy(bf16[80,136]{0,1:T(8,128)(2,1)} %param.4) | data formatting | bytes 43520 | tf_op args[1]
  2.1 129.7 %shard_map.50 = (f32[40,16,1024]{2,1,0:T(8,128)}, f32[40,16,1024]{2,1,0:T(8,128)}) custom-call(bf16[68,16,1024]{2,1,0:T(8,128)(2,1)} %inc_hbm.1, bf16[80,136]{1,0:T(8,128)(2,1)} %copy.5.proj_ref, f32[40]{0:T(128)} %helm_ref.1), custom_call_target="tpu_custom_call" | custom-call | tf_op jit(solution)/shard_map/pallas_call | solution.py:409
  131.8 0.0 copy-start
  131.8 3.7 %copy.8 = f32[40,16,1024]{2,1,0:T(8,128)} copy(f32[40,16,1024]{2,1,0:T(8,128)} %get-tuple-element.4) | data formatting | bytes 5242880
  135.5 0.0 copy-done
  135.5 1.5 %copy.9 = f32[40,16,1024]{2,1,0:T(8,128)} copy(f32[40,16,1024]{2,1,0:T(8,128)S(1)} %copy-done) | data formatting | bytes 5242880
Async XLA Ops:
  131.8 3.7 %copy-start = (f32[40,16,1024]{2,1,0:T(8,128)S(1)}, f32[40,16,1024]{2,1,0:T(8,128)}, u32[]{:S(2)}) copy-start(f32[40,16,1024]{2,1,0:T(8,128)} %get-tuple-element.5) | copy-start | bytes 7864324
where the time goes:
time: 137 us
  Pallas kernels  130 us (95%)
  local copies, waits for them, and re-layouts  6.68 us (5%)
    pallas_call x1, Pallas kernels, shards(): pl.pallas_call(functools.partial(kernel, dims), out_shape=(out, out), in_...  130 us
    unnamed x5, local copies, waits for them, and re-layouts  6.68 us

commit v1 on v0

--- a/solution.py
+++ b/solution.py
@@ -13,23 +13,18 @@
 EXT = ROWS + 2 * HALO
 NEAR = 4
 LANES = 128
-FLAT = 216
 MESH = pl.DeviceIdType.MESH
 
 
-def flat(level, row):
-    return 32 * level - level * level + row
-
-
 def kernel(dims, inc_hbm, proj_ref, helm_ref, sol_hbm, res_hbm,
-           fields, inc_own, inc_far, kron, grams, far_out, far_in, coef, gather,
+           inc_own, inc_far, kron, grams, far_out, far_in, coef, gather, sol_rows, res_rows,
            lev_send, lev_recv, load_sem, near_send, near_recv, far_send, far_recv,
-           red_send, red_recv, out_sem):
+           red_send, red_recv, out_sem, *fields):
     tile = lax.axis_index("tile")
     lev = lax.axis_index("lev")
     tiles = lax.axis_size("tile")
     levels, _, cells = inc_own.shape
-    modes = fields.shape[1]
+    modes = fields[0].shape[1]
     groups = modes // 8
     chunk = cells // 4
     cols = cells // LANES
@@ -70,17 +65,15 @@
         sends.append(send)
 
     wide = levels * ROWS
-    table = proj_ref[...].astype(f32)
-    table = jnp.where(lev == 0, table[:modes], table[modes:])
-    left, right = table[:, :levels], table[:, levels:]
-    own_part = jnp.where(lev == 0, left, right)
-    far_part = jnp.where(lev == 0, right, left)
-    spread = (lax.broadcasted_iota(jnp.int32, (levels, wide), 1) // ROWS
-              == lax.broadcasted_iota(jnp.int32, (levels, wide), 0))
-    spread = jnp.where(spread, 1.0, 0.0).astype(jnp.bfloat16)
+    table = proj_ref[...]
     at_row = lax.broadcasted_iota(jnp.int32, (modes, wide), 1) % ROWS
-    for half, part in enumerate((own_part, far_part)):
-        repeated = jnp.dot(part.astype(jnp.bfloat16), spread, preferred_element_type=f32)
+    of_level = (lax.broadcasted_iota(jnp.int32, (2 * levels, wide), 0)
+                - lax.broadcasted_iota(jnp.int32, (2 * levels, wide), 1) // ROWS)
+    for half in range(2):
+        first_level = (lev if half == 0 else other) * levels
+        spread = jnp.where(of_level == first_level, 1.0, 0.0).astype(jnp.bfloat16)
+        repeated = lax.dot_general(table, spread, (((0,), (0,)), ((), ())), preferred_element_type=f32)
+        repeated = jnp.where(lev == 0, repeated[:modes], repeated[modes:])
         for pair in range(ROWS // 2):
             both = jnp.concatenate([
                 jnp.where(at_row == 2 * pair, repeated, 0.0),
@@ -98,7 +91,7 @@
         @pl.when(jnp.logical_not(has[side]))
         def _():
             def clear(row, carry):
-                fields[row + base] = jnp.zeros((modes, cells), f32)
+                fields[0][row + base] = jnp.zeros((modes, cells), f32)
                 return carry
             lax.fori_loop(0, HALO, clear, 0)
     grams[...] = jnp.zeros_like(grams)
@@ -107,14 +100,14 @@
         loads[c].wait()
         part = pl.ds(c * chunk, chunk)
         first = jnp.dot(kron[0], inc_own[:, :, part].reshape(wide, chunk), preferred_element_type=f32)
-        fields[pl.ds(HALO, ROWS), :, part] = first.reshape(ROWS, modes, chunk)
+        fields[0][pl.ds(HALO, ROWS), :, part] = first.reshape(ROWS, modes, chunk)
 
     def near_copy(side, d, piece):
         mine = HALO + d - 1 if side == 0 else EXT - HALO - d
         theirs = EXT - HALO - 1 + d if side == 0 else HALO - d
         part = pl.ds(0, chunk) if piece == 0 else pl.ds(chunk, cells - chunk)
         return pltpu.make_async_remote_copy(
-            src_ref=fields.at[mine, :, part], dst_ref=fields.at[theirs, :, part],
+            src_ref=fields[0].at[mine, :, part], dst_ref=fields[0].at[theirs, :, part],
             send_sem=near_send.at[side, d - 1, piece], recv_sem=near_recv.at[1 - side, d - 1, piece],
             device_id={"tile": partner[side]}, device_id_type=MESH)
 
@@ -128,7 +121,7 @@
         sends[c].wait_recv()
         part = pl.ds(c * chunk, chunk)
         second = jnp.dot(kron[1], inc_far[:, :, part].reshape(wide, chunk), preferred_element_type=f32)
-        fields[pl.ds(HALO, ROWS), :, part] += second.reshape(ROWS, modes, chunk)
+        fields[0][pl.ds(HALO, ROWS), :, part] += second.reshape(ROWS, modes, chunk)
         if c in (0, 3):
             for d in range(1, NEAR + 1):
                 for side in range(2):
@@ -142,7 +135,7 @@
             for group in range(groups):
                 rows = pl.ds(8 * group, 8)
                 both = jnp.concatenate(
-                    [fields[mine, rows, pl.ds(0, half)], fields[mine, rows, pl.ds(half, half)]], axis=0)
+                    [fields[0][mine, rows, pl.ds(0, half)], fields[0][mine, rows, pl.ds(half, half)]], axis=0)
                 far_out[side, d - NEAR - 1, group] = both.astype(jnp.bfloat16)
 
             @pl.when(has[side])
@@ -152,15 +145,14 @@
     lane = lax.broadcasted_iota(jnp.int32, (modes, LANES), 1)
     at_first, at_last = lane == 0, lane == LANES - 1
 
-    def row_step(level, row, start, gram, keep=None):
-        here = flat(level - 1, row)
-        old = None if start else flat(level - 2, row)
-        new = flat(level, row)
+    def row_step(level, row, keep=None, weight=None):
+        source, new = fields[level - 1], fields[level]
+        here, there = row - (level - 1), row - level
         turned = {}
 
         def turn(j):
             if j not in turned:
-                value = fields[here, :, pl.ds(j * LANES, LANES)]
+                value = source[here, :, pl.ds(j * LANES, LANES)]
                 turned[j] = (value, pltpu.roll(value, 1, 1), pltpu.roll(value, LANES - 1, 1))
             return turned[j]
 
@@ -171,49 +163,35 @@
             before = turn(j - 1)[1] if j > 0 else 0.0
             after = turn(j + 1)[2] if j < cols - 1 else 0.0
             beside = (jnp.where(at_first, before, right_by) + jnp.where(at_last, after, left_by)
-                      + (fields[here - 1, :, part] + fields[here + 1, :, part]))
+                      + (source[here - 1, :, part] + source[here + 1, :, part]))
             result = 0.5 * beside
-            if old is not None:
-                result = result - fields[old, :, part]
+            if level > 1:
+                result = result - fields[level - 2][row - (level - 2), :, part]
             if keep is not None:
                 result = result * keep
-            fields[new, :, part] = result
-            if gram:
-                squares = value * value if squares is None else squares + value * value
-                cross = value * result if cross is None else cross + value * result
-        if gram:
-            grams[2 * level - 2] += squares
-            grams[2 * level - 1] += cross
-
-    def inner(level, start):
+            new[there, :, part] = result
+            squares = value * value if squares is None else squares + value * value
+            cross = value * result if cross is None else cross + value * result
+        if weight is not None:
+            squares, cross = squares * weight, cross * weight
+        grams[2 * level - 2] += squares
+        grams[2 * level - 1] += cross
+
+    for level in range(1, HALO):
         def pair(i, carry):
-            row = HALO + level + 2 * i
-            row_step(level, row, start, True)
-            row_step(level, row + 1, start, True)
+            row_step(level, HALO + level + 2 * i)
+            row_step(level, HALO + level + 2 * i + 1)
             return carry
         lax.fori_loop(0, HALO - level, pair, 0)
 
-    inner(1, True)
-
-    def inner_level(level, carry):
-        inner(level, False)
-        return carry
-
-    lax.fori_loop(2, HALO, inner_level, 0)
-
     keeps = tuple(jnp.where(has[side], 1.0, 0.0) for side in range(2))
-
-    def both_sides(level, d, start, gram):
-        q = level - d
-        row_step(level, HALO + q, start, gram, None if gram else keeps[0])
-        row_step(level, EXT - HALO - 1 - q, start, gram, None if gram else keeps[1])
 
     def near_wait(side, d):
         for piece in range(2):
             theirs = HALO - d if side == 0 else EXT - HALO - 1 + d
             part = pl.ds(0, chunk) if piece == 0 else pl.ds(chunk, cells - chunk)
             pltpu.make_async_remote_copy(
-                src_ref=fields.at[theirs, :, part], dst_ref=fields.at[theirs, :, part],
+                src_ref=fields[0].at[theirs, :, part], dst_ref=fields[0].at[theirs, :, part],
                 send_sem=near_send.at[side, d - 1, piece], recv_sem=near_recv.at[side, d - 1, piece],
                 device_id={"tile": partner[side]}, device_id_type=MESH).wait_recv()
 
@@ -226,8 +204,8 @@
         for group in range(groups):
             both = far_in[side, d - NEAR - 1, group].astype(f32)
             rows = pl.ds(8 * group, 8)
-            fields[theirs, rows, pl.ds(0, half)] = both[:8]
-            fields[theirs, rows, pl.ds(half, half)] = both[8:]
+            fields[0][theirs, rows, pl.ds(0, half)] = both[:8]
+            fields[0][theirs, rows, pl.ds(half, half)] = both[8:]
 
     def front(d, carry):
         for side in range(2):
@@ -239,24 +217,12 @@
             def _():
                 far_wait(side, d)
 
-        @pl.when(d == 1)
-        def _():
-            both_sides(1, d, True, True)
-
-        @pl.when(d > 1)
-        def _():
-            both_sides(1, d, True, False)
-
-        def halo_level(level, c):
-            both_sides(level, d, False, False)
-            return c
-
-        def own_level(level, c):
-            both_sides(level, d, False, True)
-            return c
-
-        lax.fori_loop(2, d, halo_level, 0)
-        lax.fori_loop(jnp.maximum(d, 2), STEPS + 1, own_level, 0)
+        top, bottom = HALO - d, EXT - HALO - 1 + d
+        for level in range(1, STEPS + 1):
+            inside = jnp.where(d <= level, 1.0, 0.0)
+            keep = [jnp.maximum(inside, keeps[side]) for side in range(2)]
+            row_step(level, top + level, keep[0], inside)
+            row_step(level, bottom - level, keep[1], inside)
         return carry
 
     lax.fori_loop(1, HALO + 1, front, 0)
@@ -347,7 +313,7 @@
             coef[i, pl.ds(8 * group, 8), :] = jnp.broadcast_to(value[:, group:group + 1], (8, LANES))
 
     def out_copy(which, row):
-        source = fields.at[flat(7 + which, HALO + row)]
+        source = (sol_rows, res_rows)[which].at[row]
         target = (sol_hbm, res_hbm)[which].at[:, row, :]
         return pltpu.make_async_copy(source, target, out_sem.at[which, row])
 
@@ -356,14 +322,14 @@
             rows = pl.ds(pl.multiple_of(8 * group, 8), 8)
             factors = [coef[i, rows, :] for i in range(2 * STEPS + 1)]
             for more in range(2):
-                row = HALO + 2 * pair + more
+                row = 2 * pair + more
                 for j in range(cols):
                     part = pl.ds(j * LANES, LANES)
-                    parts = [fields[flat(k, row), rows, part] for k in range(STEPS + 1)]
+                    parts = [fields[k][row + HALO - k, rows, part] for k in range(STEPS + 1)]
                     sol = add(factors[k] * parts[k] for k in range(STEPS))
                     res = add(factors[STEPS + k] * parts[k] for k in range(STEPS + 1))
-                    fields[flat(7, row), rows, part] = sol
-                    fields[flat(8, row), rows, part] = res
+                    sol_rows[row, rows, part] = sol
+                    res_rows[row, rows, part] = res
             return c
         lax.fori_loop(0, groups, one_group, 0)
         for more in range(2):
@@ -412,7 +378,6 @@
         in_specs=[hbm, pl.BlockSpec(memory_space=pltpu.VMEM), pl.BlockSpec(memory_space=pltpu.SMEM)],
         out_specs=(hbm, hbm),
         scratch_shapes=[
-            pltpu.VMEM((FLAT, modes, cells), jnp.float32),
             pltpu.VMEM((levels, rows, cells), jnp.bfloat16),
             pltpu.VMEM((levels, rows, cells), jnp.bfloat16),
             pltpu.VMEM((2, rows * modes, rows * levels), jnp.bfloat16),
@@ -421,15 +386,17 @@
             pltpu.VMEM((2, HALO - NEAR, groups, 16, cells // 2), jnp.bfloat16),
             pltpu.VMEM((2 * STEPS + 1, modes, LANES), jnp.float32),
             pltpu.VMEM((len(dims), longest, 8, LANES), jnp.float32),
+            pltpu.VMEM((rows, modes, cells), jnp.float32),
+            pltpu.VMEM((rows, modes, cells), jnp.float32),
             dma((4,)), dma((4,)), dma((4,)),
             dma((2, NEAR, 2)), dma((2, NEAR, 2)),
             dma((2, HALO - NEAR)), dma((2, HALO - NEAR)),
             dma((len(dims), longest - 1)), dma((len(dims), longest - 1)),
             dma((2, ROWS)),
-        ],
+        ] + [pltpu.VMEM((EXT - 2 * k, modes, cells), jnp.float32) for k in range(STEPS + 1)],
         compiler_params=pltpu.CompilerParams(
             collective_id=0, has_side_effects=True, vmem_limit_bytes=60 * 1024 * 1024),
-    )(increments, projection, helmholtz)
+    )(increments, projection.T, helmholtz)
 
 
 def solution(mesh):

time: 137 us -> 65.5 us (0.48)
  Pallas kernels: 130 us -> 59.5 us
  local copies, waits for them, and re-layouts: 6.68 us -> 5.21 us
    pallas_call x1, Pallas kernels: 130 us -> 59.5 us  [shards(): pl.pallas_call(functools.partial(kernel, dims), out_shape=(out, out), in_...]
    unnamed x5 -> x4, local copies, waits for them, and re-layouts: 6.68 us -> 5.21 us
where the time goes in v1:
time: 65.5 us; the launch traced here: 65.3 us
  Pallas kernels  59.5 us (91%)
  local copies, waits for them, and re-layouts  5.21 us (8%)
    pallas_call x1, Pallas kernels, shards(): pl.pallas_call(functools.partial(kernel, dims), out_shape=(out, out), in_...  59.5 us
    unnamed x4, local copies, waits for them, and re-layouts  5.21 us

profile of v1, /device:TPU:0, one launch (start us, length us, event | category | flops | bytes accessed | tf_op | source)
XLA Modules:
  0.0 65.3 jit_solution(2275058499209181200)
XLA Ops:
  0.6 59.5 %shard_map.50 = (f32[40,16,1024]{2,1,0:T(8,128)}, f32[40,16,1024]{2,1,0:T(8,128)}) custom-call(bf16[68,16,1024]{2,1,0:T(8,128)(2,1)} %inc_hbm.1, bf16[136,80]{1,0:T(8,128)(2,1)} %bitcast.1, f32[40]{0:T(128)} %helm_ref.1), custom_call_target="tpu_custom_call" | custom-call | tf_op jit(solution)/shard_map/pallas_call | solution.py:375
  60.1 0.0 copy-start
  60.1 3.7 %copy.7 = f32[40,16,1024]{2,1,0:T(8,128)} copy(f32[40,16,1024]{2,1,0:T(8,128)} %get-tuple-element.4) | data formatting | bytes 5242880
  63.8 0.0 copy-done
  63.8 1.5 %copy.8 = f32[40,16,1024]{2,1,0:T(8,128)} copy(f32[40,16,1024]{2,1,0:T(8,128)S(1)} %copy-done) | data formatting | bytes 5242880
Async XLA Ops:
  60.1 3.7 %copy-start = (f32[40,16,1024]{2,1,0:T(8,128)S(1)}, f32[40,16,1024]{2,1,0:T(8,128)}, u32[]{:S(2)}) copy-start(f32[40,16,1024]{2,1,0:T(8,128)} %get-tuple-element.5) | copy-start | bytes 7864324

commit v2 on v1

--- a/solution.py
+++ b/solution.py
@@ -16,10 +16,19 @@
 MESH = pl.DeviceIdType.MESH
 
 
-def kernel(dims, inc_hbm, proj_ref, helm_ref, sol_hbm, res_hbm,
-           inc_own, inc_far, kron, grams, far_out, far_in, coef, gather, sol_rows, res_rows,
-           lev_send, lev_recv, load_sem, near_send, near_recv, far_send, far_recv,
-           red_send, red_recv, out_sem, *fields):
+def add(items):
+    items = list(items)
+    while len(items) > 1:
+        items = [items[i] + items[i + 1] if i + 1 < len(items) else items[i]
+                 for i in range(0, len(items), 2)]
+    return items[0]
+
+
+def kernel(dims, inc_hbm, proj_hbm, helm_hbm, coef, *refs):
+    fields = refs[:STEPS + 1]
+    (inc_own, inc_far, kron, grams, far_out, far_in, gather,
+     lev_send, lev_recv, load_sem, near_send, near_recv, far_send, far_recv,
+     red_send, red_recv, proj_ref, helm_ref, small_sem) = refs[STEPS + 1:]
     tile = lax.axis_index("tile")
     lev = lax.axis_index("lev")
     tiles = lax.axis_size("tile")
@@ -33,18 +42,12 @@
     partner = (tile - 1, tile + 1)
     f32 = jnp.float32
 
-    loads = []
-    for c in range(4):
-        part = pl.ds(c * chunk, chunk)
-        load = pltpu.make_async_copy(inc_hbm.at[:, :, part], inc_own.at[:, :, part], load_sem.at[c])
-        load.start()
-        loads.append(load)
-
     barrier = pltpu.get_barrier_semaphore()
     pl.semaphore_signal(barrier, inc=1, device_id={"lev": other}, device_id_type=MESH)
     for side in range(2):
-        there = lax.rem(tile + (tiles - 1 if side == 0 else 1), tiles)
-        pl.semaphore_signal(barrier, inc=1, device_id={"tile": there}, device_id_type=MESH)
+        @pl.when(has[side])
+        def _():
+            pl.semaphore_signal(barrier, inc=1, device_id={"tile": partner[side]}, device_id_type=MESH)
     places = []
     for stride, size in dims:
         place = lax.rem(lax.div(tile, stride), size)
@@ -52,7 +55,20 @@
         for step in range(1, size):
             there = tile + (lax.rem(place + step, size) - place) * stride
             pl.semaphore_signal(barrier, inc=1, device_id={"tile": there}, device_id_type=MESH)
-    pl.semaphore_wait(barrier, 3 + sum(size - 1 for _, size in dims))
+
+    loads = []
+    for c in range(4):
+        part = pl.ds(c * chunk, chunk)
+        load = pltpu.make_async_copy(inc_hbm.at[:, :, part], inc_own.at[:, :, part], load_sem.at[c])
+        load.start()
+        loads.append(load)
+    small = (pltpu.make_async_copy(proj_hbm, proj_ref, small_sem.at[0]),
+             pltpu.make_async_copy(helm_hbm, helm_ref, small_sem.at[1]))
+    for load in small:
+        load.start()
+
+    peers = 1 + sum(size - 1 for _, size in dims)
+    pl.semaphore_wait(barrier, peers + sum(jnp.where(has[side], 1, 0) for side in range(2)))
 
     sends = []
     for c in range(4):
@@ -65,6 +81,8 @@
         sends.append(send)
 
     wide = levels * ROWS
+    for load in small:
+        load.wait()
     table = proj_ref[...]
     at_row = lax.broadcasted_iota(jnp.int32, (modes, wide), 1) % ROWS
     of_level = (lax.broadcasted_iota(jnp.int32, (2 * levels, wide), 0)
@@ -276,13 +294,6 @@
     r_mom, p_mom = list(moments), list(moments)
     r_co, p_co, x_co = [zero + 1.0], [zero + 1.0], []
     squares = moments[0]
-
-    def add(items):
-        items = list(items)
-        while len(items) > 1:
-            items = [items[i] + items[i + 1] if i + 1 < len(items) else items[i]
-                     for i in range(0, len(items), 2)]
-        return items[0]
 
     for step in range(STEPS):
         through = []
@@ -312,6 +323,30 @@
         for group in range(groups):
             coef[i, pl.ds(8 * group, 8), :] = jnp.broadcast_to(value[:, group:group + 1], (8, LANES))
 
+    for send in sends:
+        send.wait_send()
+    for side in range(2):
+        @pl.when(has[side])
+        def _():
+            for d in range(1, NEAR + 1):
+                for piece in range(2):
+                    near_copy(side, d, piece).wait_send()
+            for d in range(NEAR + 1, HALO + 1):
+                far_copy(side, d).wait_send()
+    for phase, (stride, size) in enumerate(dims):
+        for step in range(1, size):
+            pltpu.make_async_remote_copy(
+                src_ref=gather.at[phase, places[phase]], dst_ref=gather.at[phase, places[phase]],
+                send_sem=red_send.at[phase, step - 1], recv_sem=red_recv.at[phase, step - 1],
+                device_id={"tile": tile}, device_id_type=MESH).wait_send()
+
+
+def combine_kernel(*refs):
+    coef, fields = refs[0], refs[1:STEPS + 2]
+    sol_hbm, res_hbm, sol_rows, res_rows, out_sem = refs[STEPS + 2:]
+    groups = fields[0].shape[1] // 8
+    cols = fields[0].shape[2] // LANES
+
     def out_copy(which, row):
         source = (sol_rows, res_rows)[which].at[row]
         target = (sol_hbm, res_hbm)[which].at[:, row, :]
@@ -339,23 +374,6 @@
 
     lax.fori_loop(0, ROWS // 2, combine, 0)
 
-    for send in sends:
-        send.wait_send()
-    for side in range(2):
-        @pl.when(has[side])
-        def _():
-            for d in range(1, NEAR + 1):
-                for piece in range(2):
-                    near_copy(side, d, piece).wait_send()
-            for d in range(NEAR + 1, HALO + 1):
-                far_copy(side, d).wait_send()
-    for phase, (stride, size) in enumerate(dims):
-        for step in range(1, size):
-            pltpu.make_async_remote_copy(
-                src_ref=gather.at[phase, places[phase]], dst_ref=gather.at[phase, places[phase]],
-                send_sem=red_send.at[phase, step - 1], recv_sem=red_recv.at[phase, step - 1],
-                device_id={"tile": tile}, device_id_type=MESH).wait_send()
-
     def drain(row, carry):
         for which in range(2):
             out_copy(which, row).wait()
@@ -370,13 +388,16 @@
     groups = modes // 8
     out = jax.ShapeDtypeStruct((modes, rows, cells), jnp.float32)
     longest = max(size for _, size in dims)
-    hbm = pl.BlockSpec(memory_space=pl.ANY)
+    hbm = pl.BlockSpec(memory_space=pltpu.HBM)
     dma = pltpu.SemaphoreType.DMA
-    return pl.pallas_call(
+    vmem = pl.BlockSpec(memory_space=pltpu.VMEM)
+    kept = [pltpu.VMEM((2 * STEPS + 1, modes, LANES), jnp.float32)]
+    kept += [pltpu.VMEM((EXT - 2 * k, modes, cells), jnp.float32) for k in range(STEPS + 1)]
+    fields = pl.pallas_call(
         functools.partial(kernel, dims),
-        out_shape=(out, out),
-        in_specs=[hbm, pl.BlockSpec(memory_space=pltpu.VMEM), pl.BlockSpec(memory_space=pltpu.SMEM)],
-        out_specs=(hbm, hbm),
+        out_shape=tuple(kept),
+        in_specs=[hbm] * 3,
+        out_specs=(vmem,) * len(kept),
         scratch_shapes=[
             pltpu.VMEM((levels, rows, cells), jnp.bfloat16),
             pltpu.VMEM((levels, rows, cells), jnp.bfloat16),
@@ -384,19 +405,28 @@
             pltpu.VMEM((2 * STEPS, modes, LANES), jnp.float32),
             pltpu.VMEM((2, HALO - NEAR, groups, 16, cells // 2), jnp.bfloat16),
             pltpu.VMEM((2, HALO - NEAR, groups, 16, cells // 2), jnp.bfloat16),
-            pltpu.VMEM((2 * STEPS + 1, modes, LANES), jnp.float32),
             pltpu.VMEM((len(dims), longest, 8, LANES), jnp.float32),
-            pltpu.VMEM((rows, modes, cells), jnp.float32),
-            pltpu.VMEM((rows, modes, cells), jnp.float32),
             dma((4,)), dma((4,)), dma((4,)),
             dma((2, NEAR, 2)), dma((2, NEAR, 2)),
             dma((2, HALO - NEAR)), dma((2, HALO - NEAR)),
             dma((len(dims), longest - 1)), dma((len(dims), longest - 1)),
+            pltpu.VMEM((2 * levels, 2 * modes), jnp.bfloat16), pltpu.SMEM((modes,), jnp.float32), dma((2,)),
+        ],
+        compiler_params=pltpu.CompilerParams(
+            collective_id=0, has_side_effects=True, vmem_limit_bytes=14 * 1024 * 1024),
+    )(*(pltpu.with_memory_space_constraint(x, pltpu.HBM) for x in (increments, projection.T, helmholtz)))
+    return pl.pallas_call(
+        combine_kernel,
+        out_shape=(out, out),
+        in_specs=[vmem] * len(kept),
+        out_specs=(hbm, hbm),
+        scratch_shapes=[
+            pltpu.VMEM((rows, modes, cells), jnp.float32),
+            pltpu.VMEM((rows, modes, cells), jnp.float32),
             dma((2, ROWS)),
-        ] + [pltpu.VMEM((EXT - 2 * k, modes, cells), jnp.float32) for k in range(STEPS + 1)],
-        compiler_params=pltpu.CompilerParams(
-            collective_id=0, has_side_effects=True, vmem_limit_bytes=60 * 1024 * 1024),
-    )(increments, projection.T, helmholtz)
+        ],
+        compiler_params=pltpu.CompilerParams(vmem_limit_bytes=10 * 1024 * 1024),
+    )(*fields)
 
 
 def solution(mesh):

time: 65.5 us -> 59.4 us (0.907)
  local copies, waits for them, and re-layouts: 5.21 us -> 0 us
  Pallas kernels: 59.5 us -> 58.6 us
    unnamed x4 -> x0, local copies, waits for them, and re-layouts: 5.21 us -> none
    pallas_call x1 -> x2, Pallas kernels: 59.5 us -> 58.6 us  [the longest x1 54.3 us: shards(): pl.pallas_call(functools.partial(kernel, dims), out_shape=tuple(kept), in...]
where the time goes in v2:
time: 59.4 us; the launch traced here: 59.3 us
  Pallas kernels  58.6 us (99%)
  between operations  0.64 us (1%)
    pallas_call x1, Pallas kernels, shards(): pl.pallas_call(functools.partial(kernel, dims), out_shape=tuple(kept), in...  54.3 us
    pallas_call x1, Pallas kernels, shards(): pl.pallas_call(combine_kernel, out_shape=(out, out), in_specs=[vmem] * le...  4.36 us

profile of v2, /device:TPU:0, one launch (start us, length us, event | category | flops | bytes accessed | tf_op | source)
XLA Modules:
  0.0 59.3 jit_solution(12495237028858754743)
XLA Ops:
  0.6 54.3 %shard_map.50 = (f32[17,40,128]{2,1,0:T(8,128)S(1)}, f32[32,40,1024]{2,1,0:T(8,128)S(1)}, f32[30,40,1024]{2,1,0:T(8,128)S(1)}, f32[28,40,1024]{2,1,0:T(8,128)S(1...) custom-call(bf16[68,16,1024]{2,1,0:T(8,128)(2,1)} %inc_hbm.1, ...), custom_call_target="tpu_custom_call" | custom-call | tf_op jit(solution)/shard_map/pallas_call | solution.py:396
  54.9 4.4 %shard_map.51 = (f32[40,16,1024]{2,1,0:T(8,128)}, f32[40,16,1024]{2,1,0:T(8,128)}) custom-call(f32[17,40,128]{2,1,0:T(8,128)S(1)} %get-tuple-element.12.refs_0_, f32[32,40,1024]{2,1,0:T(8,128)S(1)} %get-tuple-element.13.refs_1_, f32[30,40,1024]{2,1,0:T(8,128)S(1)} %get-tuple-element.14.refs_2_, f32[28,40,1024]{2,1,0:T(8,128)S(1)} %get-tuple-element.15.refs_3_, ...), custom_call_target="tpu_custom_call" | custom-call | tf_op jit(solution)/shard_map/pallas_call | solution.py:418

commit v3 on v2

--- a/solution.py
+++ b/solution.py
@@ -28,7 +28,7 @@
     fields = refs[:STEPS + 1]
     (inc_own, inc_far, kron, grams, far_out, far_in, gather,
      lev_send, lev_recv, load_sem, near_send, near_recv, far_send, far_recv,
-     red_send, red_recv, proj_ref, helm_ref, small_sem) = refs[STEPS + 1:]
+     red_send, red_recv, proj_ref, helm_ref, small_sem, relay_sem) = refs[STEPS + 1:]
     tile = lax.axis_index("tile")
     lev = lax.axis_index("lev")
     tiles = lax.axis_size("tile")
@@ -44,8 +44,12 @@
 
     barrier = pltpu.get_barrier_semaphore()
     pl.semaphore_signal(barrier, inc=1, device_id={"lev": other}, device_id_type=MESH)
+    block = dims[2][0]
+    corner = dims[1][0] * (dims[1][1] - 1)
+    spot = lax.rem(tile, block)
+    close = (spot != 0, spot != block - 1)
     for side in range(2):
-        @pl.when(has[side])
+        @pl.when(close[side])
         def _():
             pl.semaphore_signal(barrier, inc=1, device_id={"tile": partner[side]}, device_id_type=MESH)
     places = []
@@ -68,7 +72,7 @@
         load.start()
 
     peers = 1 + sum(size - 1 for _, size in dims)
-    pl.semaphore_wait(barrier, peers + sum(jnp.where(has[side], 1, 0) for side in range(2)))
+    pl.semaphore_wait(barrier, peers + sum(jnp.where(close[side], 1, 0) for side in range(2)))
 
     sends = []
     for c in range(4):
@@ -79,6 +83,21 @@
             device_id={"lev": other}, device_id_type=MESH)
         send.start()
         sends.append(send)
+
+    inner = tile + block < tiles
+    ends = ((spot == block - 1) & inner, (spot == 0) & (tile > 0))
+    relays = ((spot == corner) & inner, (spot == 0) & inner)
+
+    def pass_on(condition, arrives, leaves, there):
+        @pl.when(condition)
+        def _():
+            if arrives is not None:
+                pl.semaphore_wait(relay_sem.at[arrives], 1)
+            if leaves is not None:
+                pl.semaphore_signal(relay_sem.at[leaves], inc=1, device_id={"tile": there}, device_id_type=MESH)
+
+    pass_on(ends[1], None, 0, tile - block)
+    pass_on(ends[0], None, 3, tile - (block - 1 - corner))
 
     wide = levels * ROWS
     for load in small:
@@ -98,6 +117,9 @@
                 jnp.where(at_row == 2 * pair + 1, repeated, 0.0)], axis=0)
             kron[half, pl.ds(2 * modes * pair, 2 * modes), :] = both.astype(jnp.bfloat16)
 
+    pass_on(relays[1], 0, 1, tile + corner)
+    pass_on(relays[0], 3, 4, tile - corner)
+
     lane8 = lax.broadcasted_iota(jnp.int32, (8, LANES), 1)
     sub8 = lax.broadcasted_iota(jnp.int32, (8, LANES), 0)
     shifts = jnp.zeros((8, LANES), f32)
@@ -120,6 +142,9 @@
         first = jnp.dot(kron[0], inc_own[:, :, part].reshape(wide, chunk), preferred_element_type=f32)
         fields[0][pl.ds(HALO, ROWS), :, part] = first.reshape(ROWS, modes, chunk)
 
+    pass_on(relays[0], 1, 2, tile + (block - 1 - corner))
+    pass_on(relays[1], 4, 5, tile + block)
+
     def near_copy(side, d, piece):
         mine = HALO + d - 1 if side == 0 else EXT - HALO - d
         theirs = EXT - HALO - 1 + d if side == 0 else HALO - d
@@ -140,6 +165,9 @@
         part = pl.ds(c * chunk, chunk)
         second = jnp.dot(kron[1], inc_far[:, :, part].reshape(wide, chunk), preferred_element_type=f32)
         fields[0][pl.ds(HALO, ROWS), :, part] += second.reshape(ROWS, modes, chunk)
+        if c == 0:
+            pass_on(ends[0], 2, None, None)
+            pass_on(ends[1], 5, None, None)
         if c in (0, 3):
             for d in range(1, NEAR + 1):
                 for side in range(2):
@@ -163,7 +191,7 @@
     lane = lax.broadcasted_iota(jnp.int32, (modes, LANES), 1)
     at_first, at_last = lane == 0, lane == LANES - 1
 
-    def row_step(level, row, keep=None, weight=None):
+    def row_step(level, row, keep=None, gram=True):
         source, new = fields[level - 1], fields[level]
         here, there = row - (level - 1), row - level
         turned = {}
@@ -188,12 +216,12 @@
             if keep is not None:
                 result = result * keep
             new[there, :, part] = result
-            squares = value * value if squares is None else squares + value * value
-            cross = value * result if cross is None else cross + value * result
-        if weight is not None:
-            squares, cross = squares * weight, cross * weight
-        grams[2 * level - 2] += squares
-        grams[2 * level - 1] += cross
+            if gram:
+                squares = value * value if squares is None else squares + value * value
+                cross = value * result if cross is None else cross + value * result
+        if gram:
+            grams[2 * level - 2] += squares
+            grams[2 * level - 1] += cross
 
     for level in range(1, HALO):
         def pair(i, carry):
@@ -225,25 +253,20 @@
             fields[0][theirs, rows, pl.ds(0, half)] = both[:8]
             fields[0][theirs, rows, pl.ds(half, half)] = both[8:]
 
-    def front(d, carry):
+    def front(d):
         for side in range(2):
-            @pl.when(has[side] & (d <= NEAR))
+            @pl.when(has[side])
             def _():
-                near_wait(side, d)
-
-            @pl.when(has[side] & (d > NEAR))
-            def _():
-                far_wait(side, d)
+                (near_wait if d <= NEAR else far_wait)(side, d)
 
         top, bottom = HALO - d, EXT - HALO - 1 + d
         for level in range(1, STEPS + 1):
-            inside = jnp.where(d <= level, 1.0, 0.0)
-            keep = [jnp.maximum(inside, keeps[side]) for side in range(2)]
-            row_step(level, top + level, keep[0], inside)
-            row_step(level, bottom - level, keep[1], inside)
-        return carry
-
-    lax.fori_loop(1, HALO + 1, front, 0)
+            inside = d <= level
+            row_step(level, top + level, None if inside else keeps[0], inside)
+            row_step(level, bottom - level, None if inside else keeps[1], inside)
+
+    for d in range(1, HALO + 1):
+        front(d)
 
     values = [grams[i] for i in range(2 * STEPS)]
 
@@ -411,6 +434,7 @@
             dma((2, HALO - NEAR)), dma((2, HALO - NEAR)),
             dma((len(dims), longest - 1)), dma((len(dims), longest - 1)),
             pltpu.VMEM((2 * levels, 2 * modes), jnp.bfloat16), pltpu.SMEM((modes,), jnp.float32), dma((2,)),
+            pltpu.SemaphoreType.REGULAR((6,)),
         ],
         compiler_params=pltpu.CompilerParams(
             collective_id=0, has_side_effects=True, vmem_limit_bytes=14 * 1024 * 1024),

time: 59.4 us -> 56.2 us (0.946)
  Pallas kernels: 58.6 us -> 55.2 us
    pallas_call x1, Pallas kernels: 54.3 us -> 50.9 us  [shards(): pl.pallas_call(functools.partial(kernel, dims), out_shape=tuple(kept), in...]
where the time goes in v3:
time: 56.2 us; the launch traced here: 56 us
  Pallas kernels  55.2 us (98%)
  between operations  0.82 us (1%)
    pallas_call x1, Pallas kernels, shards(): pl.pallas_call(functools.partial(kernel, dims), out_shape=tuple(kept), in...  50.9 us
    pallas_call x1, Pallas kernels, shards(): pl.pallas_call(combine_kernel, out_shape=(out, out), in_specs=[vmem] * le...  4.36 us

profile of v3, /device:TPU:0, one launch (start us, length us, event | category | flops | bytes accessed | tf_op | source)
XLA Modules:
  0.0 56.0 jit_solution(5734177966861625443)
XLA Ops:
  0.6 50.9 %shard_map.50 = (f32[17,40,128]{2,1,0:T(8,128)S(1)}, f32[32,40,1024]{2,1,0:T(8,128)S(1)}, f32[30,40,1024]{2,1,0:T(8,128)S(1)}, f32[28,40,1024]{2,1,0:T(8,128)S(1...) custom-call(bf16[68,16,1024]{2,1,0:T(8,128)(2,1)} %inc_hbm.1, ...), custom_call_target="tpu_custom_call" | custom-call | tf_op jit(solution)/shard_map/pallas_call | solution.py:419
  51.5 4.4 %shard_map.51 = (f32[40,16,1024]{2,1,0:T(8,128)}, f32[40,16,1024]{2,1,0:T(8,128)}) custom-call(f32[17,40,128]{2,1,0:T(8,128)S(1)} %get-tuple-element.12.refs_0_, f32[32,40,1024]{2,1,0:T(8,128)S(1)} %get-tuple-element.13.refs_1_, f32[30,40,1024]{2,1,0:T(8,128)S(1)} %get-tuple-element.14.refs_2_, f32[28,40,1024]{2,1,0:T(8,128)S(1)} %get-tuple-element.15.refs_3_, ...), custom_call_target="tpu_custom_call" | custom-call | tf_op jit(solution)/shard_map/pallas_call | solution.py:442

commit v4 on v3

--- a/solution.py
+++ b/solution.py
@@ -71,34 +71,13 @@
     for load in small:
         load.start()
 
-    peers = 1 + sum(size - 1 for _, size in dims)
-    pl.semaphore_wait(barrier, peers + sum(jnp.where(close[side], 1, 0) for side in range(2)))
-
-    sends = []
-    for c in range(4):
-        part = pl.ds(c * chunk, chunk)
-        send = pltpu.make_async_remote_copy(
-            src_ref=inc_hbm.at[:, :, part], dst_ref=inc_far.at[:, :, part],
-            send_sem=lev_send.at[c], recv_sem=lev_recv.at[c],
-            device_id={"lev": other}, device_id_type=MESH)
-        send.start()
-        sends.append(send)
-
-    inner = tile + block < tiles
-    ends = ((spot == block - 1) & inner, (spot == 0) & (tile > 0))
-    relays = ((spot == corner) & inner, (spot == 0) & inner)
-
-    def pass_on(condition, arrives, leaves, there):
-        @pl.when(condition)
+    for side, base in ((0, 0), (1, EXT - HALO)):
+        @pl.when(jnp.logical_not(has[side]))
         def _():
-            if arrives is not None:
-                pl.semaphore_wait(relay_sem.at[arrives], 1)
-            if leaves is not None:
-                pl.semaphore_signal(relay_sem.at[leaves], inc=1, device_id={"tile": there}, device_id_type=MESH)
-
-    pass_on(ends[1], None, 0, tile - block)
-    pass_on(ends[0], None, 3, tile - (block - 1 - corner))
-
+            def clear(row, carry):
+                fields[0][row + base] = jnp.zeros((modes, cells), f32)
+                return carry
+            lax.fori_loop(0, HALO, clear, 0)
     wide = levels * ROWS
     for load in small:
         load.wait()
@@ -117,9 +96,6 @@
                 jnp.where(at_row == 2 * pair + 1, repeated, 0.0)], axis=0)
             kron[half, pl.ds(2 * modes * pair, 2 * modes), :] = both.astype(jnp.bfloat16)
 
-    pass_on(relays[1], 0, 1, tile + corner)
-    pass_on(relays[0], 3, 4, tile - corner)
-
     lane8 = lax.broadcasted_iota(jnp.int32, (8, LANES), 1)
     sub8 = lax.broadcasted_iota(jnp.int32, (8, LANES), 0)
     shifts = jnp.zeros((8, LANES), f32)
@@ -127,16 +103,40 @@
         shifts = jnp.where((lane8 == mode // 8) & (sub8 == mode % 8), helm_ref[mode], shifts)
     scale = 4.0 / (4.0 + shifts)
 
-    for side, base in ((0, 0), (1, EXT - HALO)):
-        @pl.when(jnp.logical_not(has[side]))
+    grams[...] = jnp.zeros_like(grams)
+
+    peers = 1 + sum(size - 1 for _, size in dims)
+    pl.semaphore_wait(barrier, peers + sum(jnp.where(close[side], 1, 0) for side in range(2)))
+
+    sends = []
+    for c in range(4):
+        part = pl.ds(c * chunk, chunk)
+        send = pltpu.make_async_remote_copy(
+            src_ref=inc_hbm.at[:, :, part], dst_ref=inc_far.at[:, :, part],
+            send_sem=lev_send.at[c], recv_sem=lev_recv.at[c],
+            device_id={"lev": other}, device_id_type=MESH)
+        send.start()
+        sends.append(send)
+
+    inner = tile + block < tiles
+    ends = ((spot == block - 1) & inner, (spot == 0) & (tile > 0))
+    relays = ((spot == corner) & inner, (spot == 0) & inner)
+
+    def pass_on(condition, arrives, leaves, there):
+        @pl.when(condition)
         def _():
-            def clear(row, carry):
-                fields[0][row + base] = jnp.zeros((modes, cells), f32)
-                return carry
-            lax.fori_loop(0, HALO, clear, 0)
-    grams[...] = jnp.zeros_like(grams)
+            if arrives is not None:
+                pl.semaphore_wait(relay_sem.at[arrives], 1)
+            if leaves is not None:
+                pl.semaphore_signal(relay_sem.at[leaves], inc=1, device_id={"tile": there}, device_id_type=MESH)
+
+    pass_on(ends[1], None, 0, tile - block)
+    pass_on(ends[0], None, 3, tile - (block - 1 - corner))
 
     for c in range(4):
+        if c == 2:
+            pass_on(relays[1], 0, 1, tile + corner)
+            pass_on(relays[0], 3, 4, tile - corner)
         loads[c].wait()
         part = pl.ds(c * chunk, chunk)
         first = jnp.dot(kron[0], inc_own[:, :, part].reshape(wide, chunk), preferred_element_type=f32)
@@ -224,11 +224,17 @@
             grams[2 * level - 1] += cross
 
     for level in range(1, HALO):
-        def pair(i, carry):
-            row_step(level, HALO + level + 2 * i)
-            row_step(level, HALO + level + 2 * i + 1)
+        pairs = HALO - level
+
+        def four(i, carry):
+            for more in range(4):
+                row_step(level, HALO + level + 4 * i + more)
             return carry
-        lax.fori_loop(0, HALO - level, pair, 0)
+
+        lax.fori_loop(0, pairs // 2, four, 0)
+        if pairs % 2:
+            for more in range(2):
+                row_step(level, HALO + level + 2 * pairs - 2 + more)
 
     keeps = tuple(jnp.where(has[side], 1.0, 0.0) for side in range(2))
 

time: 56.2 us -> 55.1 us (0.980)
  Pallas kernels: 55.2 us -> 54.1 us
    pallas_call x1, Pallas kernels: 50.9 us -> 49.7 us  [shards(): pl.pallas_call(functools.partial(kernel, dims), out_shape=tuple(kept), in...]
where the time goes in v4:
time: 55.1 us; the launch traced here: 54.9 us
  Pallas kernels  54.1 us (98%)
  between operations  0.82 us (1%)
    pallas_call x1, Pallas kernels, shards(): pl.pallas_call(functools.partial(kernel, dims), out_shape=tuple(kept), in...  49.7 us
    pallas_call x1, Pallas kernels, shards(): pl.pallas_call(combine_kernel, out_shape=(out, out), in_specs=[vmem] * le...  4.36 us

profile of v4, /device:TPU:0, one launch (start us, length us, event | category | flops | bytes accessed | tf_op | source)
XLA Modules:
  0.0 54.9 jit_solution(6513463537839065917)
XLA Ops:
  0.6 49.7 %shard_map.50 = (f32[17,40,128]{2,1,0:T(8,128)S(1)}, f32[32,40,1024]{2,1,0:T(8,128)S(1)}, f32[30,40,1024]{2,1,0:T(8,128)S(1)}, f32[28,40,1024]{2,1,0:T(8,128)S(1...) custom-call(bf16[68,16,1024]{2,1,0:T(8,128)(2,1)} %inc_hbm.1, ...), custom_call_target="tpu_custom_call" | custom-call | tf_op jit(solution)/shard_map/pallas_call | solution.py:425
  50.4 4.4 %shard_map.51 = (f32[40,16,1024]{2,1,0:T(8,128)}, f32[40,16,1024]{2,1,0:T(8,128)}) custom-call(f32[17,40,128]{2,1,0:T(8,128)S(1)} %get-tuple-element.12.refs_0_, f32[32,40,1024]{2,1,0:T(8,128)S(1)} %get-tuple-element.13.refs_1_, f32[30,40,1024]{2,1,0:T(8,128)S(1)} %get-tuple-element.14.refs_2_, f32[28,40,1024]{2,1,0:T(8,128)S(1)} %get-tuple-element.15.refs_3_, ...), custom_call_target="tpu_custom_call" | custom-call | tf_op jit(solution)/shard_map/pallas_call | solution.py:448

commit v5 on v4

--- a/solution.py
+++ b/solution.py
@@ -191,7 +191,7 @@
     lane = lax.broadcasted_iota(jnp.int32, (modes, LANES), 1)
     at_first, at_last = lane == 0, lane == LANES - 1
 
-    def row_step(level, row, keep=None, gram=True):
+    def row_step(level, row, keep=None, gram=True, stage="all", outward=0):
         source, new = fields[level - 1], fields[level]
         here, there = row - (level - 1), row - level
         turned = {}
@@ -205,21 +205,28 @@
         squares = cross = None
         for j in range(cols):
             part = pl.ds(j * LANES, LANES)
-            value, right_by, left_by = turn(j)
-            before = turn(j - 1)[1] if j > 0 else 0.0
-            after = turn(j + 1)[2] if j < cols - 1 else 0.0
-            beside = (jnp.where(at_first, before, right_by) + jnp.where(at_last, after, left_by)
-                      + (source[here - 1, :, part] + source[here + 1, :, part]))
-            result = 0.5 * beside
-            if level > 1:
-                result = result - fields[level - 2][row - (level - 2), :, part]
-            if keep is not None:
+            if stage == "finish":
+                value = source[here, :, part]
+                result = new[there, :, part] + 0.5 * source[here + outward, :, part]
+            else:
+                value, right_by, left_by = turn(j)
+                before = turn(j - 1)[1] if j > 0 else 0.0
+                after = turn(j + 1)[2] if j < cols - 1 else 0.0
+                beside = jnp.where(at_first, before, right_by) + jnp.where(at_last, after, left_by)
+                if stage == "all":
+                    beside = beside + (source[here - 1, :, part] + source[here + 1, :, part])
+                else:
+                    beside = beside + source[here - outward, :, part]
+                result = 0.5 * beside
+                if level > 1:
+                    result = result - fields[level - 2][row - (level - 2), :, part]
+            if keep is not None and stage != "ahead":
                 result = result * keep
             new[there, :, part] = result
-            if gram:
+            if gram and stage != "ahead":
                 squares = value * value if squares is None else squares + value * value
                 cross = value * result if cross is None else cross + value * result
-        if gram:
+        if gram and stage != "ahead":
             grams[2 * level - 2] += squares
             grams[2 * level - 1] += cross
 
@@ -260,16 +267,21 @@
             fields[0][theirs, rows, pl.ds(half, half)] = both[8:]
 
     def front(d):
+        top, bottom = HALO - d, EXT - HALO - 1 + d
+        last = d == HALO
+        if last:
+            for level in range(1, STEPS + 1):
+                row_step(level, top + level, stage="ahead", outward=-1)
+                row_step(level, bottom - level, stage="ahead", outward=1)
         for side in range(2):
             @pl.when(has[side])
             def _():
                 (near_wait if d <= NEAR else far_wait)(side, d)
-
-        top, bottom = HALO - d, EXT - HALO - 1 + d
         for level in range(1, STEPS + 1):
             inside = d <= level
-            row_step(level, top + level, None if inside else keeps[0], inside)
-            row_step(level, bottom - level, None if inside else keeps[1], inside)
+            stage = "finish" if last else "all"
+            row_step(level, top + level, None if inside else keeps[0], inside, stage, -1)
+            row_step(level, bottom - level, None if inside else keeps[1], inside, stage, 1)
 
     for d in range(1, HALO + 1):
         front(d)

time: 55.1 us -> 55.3 us (level)
  no operation moved by 1% of the time
where the time goes in v5:
time: 55.3 us; the launch traced here: 55.1 us
  Pallas kernels  54.3 us (98%)
  between operations  0.82 us (1%)
    pallas_call x1, Pallas kernels, shards(): pl.pallas_call(functools.partial(kernel, dims), out_shape=tuple(kept), in...  50 us
    pallas_call x1, Pallas kernels, shards(): pl.pallas_call(combine_kernel, out_shape=(out, out), in_specs=[vmem] * le...  4.36 us

profile of v5, /device:TPU:0, one launch (start us, length us, event | category | flops | bytes accessed | tf_op | source)
XLA Modules:
  0.0 55.1 jit_solution(15298075296785624854)
XLA Ops:
  0.6 50.0 %shard_map.50 = (f32[17,40,128]{2,1,0:T(8,128)S(1)}, f32[32,40,1024]{2,1,0:T(8,128)S(1)}, f32[30,40,1024]{2,1,0:T(8,128)S(1)}, f32[28,40,1024]{2,1,0:T(8,128)S(1...) custom-call(bf16[68,16,1024]{2,1,0:T(8,128)(2,1)} %inc_hbm.1, ...), custom_call_target="tpu_custom_call" | custom-call | tf_op jit(solution)/shard_map/pallas_call | solution.py:437
  50.6 4.4 %shard_map.51 = (f32[40,16,1024]{2,1,0:T(8,128)}, f32[40,16,1024]{2,1,0:T(8,128)}) custom-call(f32[17,40,128]{2,1,0:T(8,128)S(1)} %get-tuple-element.12.refs_0_, f32[32,40,1024]{2,1,0:T(8,128)S(1)} %get-tuple-element.13.refs_1_, f32[30,40,1024]{2,1,0:T(8,128)S(1)} %get-tuple-element.14.refs_2_, f32[28,40,1024]{2,1,0:T(8,128)S(1)} %get-tuple-element.15.refs_3_, ...), custom_call_target="tpu_custom_call" | custom-call | tf_op jit(solution)/shard_map/pallas_call | solution.py:460
